TPU v7x, 32 devices: a whole 2x2x4 slice. The times are simulated.
32 devices in a mesh: row: 4 (over z), col: 8 (over y, x, core).
Axes of the slice: x: 2, y: 2, z: 4, core: 2. Of those that a mesh axis runs over, the one named last changes fastest.
Arguments:
- exchange_k: float32 [16, 16, 128, 128], P('row', 'col'), may hold values from -6 to 6
- margins: bfloat16 [16, 16, 2, 8, 128, 128], P('row', 'col'), may hold values from -0.5 to 0.5
- pno_energy: float32 [16, 16, 128], P('row', 'col'), may hold values from 0.4 to 4
- pno_count: int32 [16, 16], P('row', 'col'), may hold values from 64 to 128
- occ_energy: float32 [16], replicated, may hold values from -1.5 to -0.3
- coupling: float32 [16, 8], replicated, may hold values from -0.15 to 0.15
- neighbours: int32 [16, 8], replicated, may hold values from 0 to 15, as said below
Outputs:
- amplitudes: float32 [16, 16, 128, 128], P('row', 'col')
- residual: float32 [16, 16, 128, 128], P('row', 'col')
Inputs may be any that keep to these rules, and one draw needn't show every extreme that they name: `neighbours`: row i lists 8 different orbitals k, none equal to i, each within 6 positions of i counted cyclically modulo 16.
All inputs are finite; a program needn't handle non-finite values.
Results may differ from a plain program's by a relative error of at most 0.00045.
Values may be sent and summed in bfloat16 or wider, within the bound.
A program may use at most 128 MiB of HBM per device.

v0:
```python
import jax
import jax.numpy as jnp
from jax import lax
from jax.sharding import PartitionSpec as P

REACH = 6
ITERS = 3


def from_behind(value, axis, by):
    peers = lax.axis_size(axis)
    return lax.ppermute(value, axis, [(i, (i + by) % peers) for i in range(peers)])


def rim_positions(listed, start_at, amount, orbitals):
    owners = start_at + jnp.arange(amount, dtype=jnp.int32)
    offset = (listed - owners[:, None] + orbitals) % orbitals
    offset = jnp.where(offset > orbitals // 2, offset - orbitals, offset)
    return jnp.arange(amount, dtype=jnp.int32)[:, None] + REACH + offset


def distances(amount):
    reach_shards = (REACH + amount - 1) // amount
    return (reach_shards, list(range(reach_shards, 0, -1)) + list(range(-1, -reach_shards - 1, -1)))


def rims_rows(rounded):
    amount = rounded.shape[0]
    reach_shards, steps_list = distances(amount)
    fetched = {}
    for step_by in steps_list:
        fetched[step_by] = from_behind(rounded, "row", step_by)
    lower = [fetched[step_by] for step_by in range(reach_shards, 0, -1)]
    upper = [fetched[-step_by] for step_by in range(1, reach_shards + 1)]
    joined = jnp.concatenate(lower + [rounded] + upper, axis=0)
    begin = reach_shards * amount - REACH
    return joined[begin : begin + amount + 2 * REACH]


def rims_cols(rounded):
    amount = rounded.shape[1]
    reach_shards, steps_list = distances(amount)
    fetched = {}
    for step_by in steps_list:
        fetched[step_by] = from_behind(rounded, "col", step_by)
    lower = [fetched[step_by] for step_by in range(reach_shards, 0, -1)]
    upper = [fetched[-step_by] for step_by in range(1, reach_shards + 1)]
    joined = jnp.concatenate(lower + [rounded] + upper, axis=1)
    begin = reach_shards * amount - REACH
    return joined


def mirror(updated):
    spread = lax.all_to_all(updated, "col", split_axis=2, concat_axis=1, tiled=True)
    gathered = lax.all_to_all(
        lax.all_to_all(spread, "row", split_axis=1, concat_axis=0, tiled=True),
        "col",
        split_axis=0,
        concat_axis=2,
        tiled=True,
    )
    return jnp.transpose(gathered, (1, 0, 3, 2))


def per_device(exchange_k, margins, pno_energy, pno_count, occ_energy, coupling, neighbours):
    row_count = exchange_k.shape[0]
    col_count = exchange_k.shape[1]
    pno_width = exchange_k.shape[2]
    orbitals = neighbours.shape[0]
    row_start = lax.axis_index("row") * row_count
    col_start = lax.axis_index("col") * col_count
    occ_rows = lax.dynamic_slice_in_dim(occ_energy, row_start, row_count, 0)
    occ_cols = lax.dynamic_slice_in_dim(occ_energy, col_start, col_count, 0)
    lists_rows = lax.dynamic_slice_in_dim(neighbours, row_start, row_count, 0)
    lists_cols = lax.dynamic_slice_in_dim(neighbours, col_start, col_count, 0)
    weight_rows = lax.dynamic_slice_in_dim(coupling, row_start, row_count, 0)
    weight_cols = lax.dynamic_slice_in_dim(coupling, col_start, col_count, 0)
    place_rows = rim_positions(lists_rows, row_start, row_count, orbitals)
    place_cols = rim_positions(lists_cols, col_start, col_count, orbitals)
    levels = jnp.arange(pno_width, dtype=jnp.int32)
    living = (levels[None, None, :] < pno_count[:, :, None]).astype(jnp.float32)
    pair_mask = living[:, :, :, None] * living[:, :, None, :]
    denominator = (
        pno_energy[:, :, :, None]
        + pno_energy[:, :, None, :]
        - occ_rows[:, None, None, None]
        - occ_cols[None, :, None, None]
    )
    side_rows = margins[:, :, 0]
    side_cols = margins[:, :, 1]
    amplitudes = jnp.zeros(exchange_k.shape, jnp.float32)
    residual = exchange_k
    for sweep_index in range(ITERS):
        if sweep_index > 0:
            rounded = amplitudes.astype(jnp.bfloat16)
            rows_wide = rims_rows(rounded)
            cols_wide = rims_cols(rounded)
            near_rows = rows_wide[place_rows]
            near_cols = cols_wide[:, place_cols]
            half_rows = jnp.einsum(
                "ijmab,imjbc->ijmac", side_rows, near_rows, preferred_element_type=jnp.float32
            ).astype(jnp.bfloat16)
            full_rows = jnp.einsum(
                "ijmac,ijmdc->ijmad", half_rows, side_rows, preferred_element_type=jnp.float32
            )
            half_cols = jnp.einsum(
                "ijmab,ijmbc->ijmac", side_cols, near_cols, preferred_element_type=jnp.float32
            ).astype(jnp.bfloat16)
            full_cols = jnp.einsum(
                "ijmac,ijmdc->ijmad", half_cols, side_cols, preferred_element_type=jnp.float32
            )
            coupled = jnp.sum(full_rows * weight_rows[:, None, :, None, None], axis=2) + jnp.sum(
                full_cols * weight_cols[None, :, :, None, None], axis=2
            )
        else:
            coupled = jnp.zeros(exchange_k.shape, jnp.float32)
        residual = exchange_k + denominator * amplitudes - coupled
        updated = pair_mask * (amplitudes - residual / denominator)
        amplitudes = pair_mask * (0.5 * (updated + mirror(updated)))
    return (amplitudes, residual)


def solution(mesh):
    return jax.shard_map(
        per_device,
        mesh=mesh,
        in_specs=(
            P("row", "col", None, None),
            P("row", "col", None, None, None, None),
            P("row", "col", None),
            P("row", "col"),
            P(),
            P(),
            P(),
        ),
        out_specs=(P("row", "col", None, None), P("row", "col", None, None)),
        check_vma=False,
    )
```

profile of v0, /device:TPU:3, one launch (start us, length us, event | category | flops | bytes accessed | tf_op | source)
XLA Modules:
  0.0 244.4 jit_solution(6605534473711116884)
XLA Ops:
  0.7 0.7 dynamic_slice.19
  1.4 0.7 dynamic_slice.18
  2.1 0.8 copy.142
  3.0 1.4 multiply_multiply_fusion.5
  4.8 12.4 %all_to_all.162 = f32[4,2,128,128]{3,1,0,2:T(2,128)S(1)} all-to-all(f32[4,2,128,128]{3,1,0,2:T(2,128)S(1)} %copy.143), channel_id=1, replica_groups=mesh['row'=4,'col'=8] {'col'}, dimensions={2} | all-to-all | bytes 1048576 | tf_op jit(solution)/shard_map/all_to_all | solution.py:54
  17.3 0.8 copy.146
  18.2 4.6 %all-to-all-start.1 = ((f32[4,16,16,128]{3,2,0,1:T(8,128)}), f32[4,16,16,128]{3,2,0,1:T(8,128)S(1)}, u32[]{:S(2)}, u32[]{:S(2)}) async-start(f32[4,16,16,128]{3,2,0,1:T(8,128)} %copy.146), calls=%async_computation.1 | async-start | bytes 1048576 | tf_op jit(solution)/shard_map/all_to_all | solution.py:56
  22.8 14.0 %all-to-all-done.1 = f32[4,16,16,128]{3,2,0,1:T(8,128)S(1)} async-done(((f32[4,16,16,128]{3,2,0,1:T(8,128)}), f32[4,16,16,128]{3,2,0,1:T(8,128)S(1)}, u32[]{:S(2)}, u32[]{:S(2)}) %all-to-all-start.1) | async-done | bytes 524320 | tf_op jit(solution)/shard_map/all_to_all | solution.py:56
  36.8 0.9 copy.148
  37.7 5.3 %all-to-all-start.2 = ((f32[16,4,16,128]{3,2,1,0:T(8,128)}), f32[16,4,16,128]{3,2,1,0:T(8,128)S(1)}, u32[]{:S(2)}, u32[]{:S(2)}) async-start(f32[16,4,16,128]{3,2,1,0:T(8,128)} %bitcast.6), calls=%async_computation.2 | async-start | bytes 1048576 | tf_op jit(solution)/shard_map/all_to_all | solution.py:55
  43.1 8.0 %all-to-all-done.2 = f32[16,4,16,128]{3,2,1,0:T(8,128)S(1)} async-done(((f32[16,4,16,128]{3,2,1,0:T(8,128)}), f32[16,4,16,128]{3,2,1,0:T(8,128)S(1)}, u32[]{:S(2)}, u32[]{:S(2)}) %all-to-all-start.2) | async-done | bytes 524320 | tf_op jit(solution)/shard_map/all_to_all | solution.py:55
  51.8 0.7 collective-permute-start.3
  52.9 2.1 collective-permute-start.4
  55.1 1.5 collective-permute-start.1
  56.6 3.7 %collective-permute-done.3 = bf16[4,2,128,128]{3,2,1,0:T(8,128)(2,1)S(1)} collective-permute-done((bf16[4,2,128,128]{3,2,1,0:T(8,128)(2,1)S(1)}, bf16[4,2,128,128]{3,2,1,0:T(8,128)(2,1)S(1)}, u32[]{:S(2)}, u32[]{:S(2)}) %collective-permute-start.3) | collective-permute-done | bytes 262176 | tf_op jit(solution)/shard_map/ppermute | solution.py:12
  60.3 1.2 collective-permute-start.2
  61.4 0.8 constant_dynamic-update-slice_fusion.11
  62.2 9.8 %collective-permute-done = bf16[4,2,128,128]{3,2,1,0:T(8,128)(2,1)S(1)} collective-permute-done((bf16[4,2,128,128]{3,2,1,0:T(8,128)(2,1)S(1)}, bf16[4,2,128,128]{3,2,1,0:T(8,128)(2,1)S(1)}, u32[]{:S(2)}, u32[]{:S(2)}) %collective-permute-start) | collective-permute-done | bytes 262176 | tf_op jit(solution)/shard_map/ppermute | solution.py:12
  72.5 1.2 collective-permute-start.7
  73.7 0.7 constant_dynamic-update-slice_fusion.10
  74.5 1.6 collective-permute-start.8
  76.0 0.7 constant_dynamic-update-slice_fusion.9
  76.8 0.8 constant_dynamic-update-slice_fusion.8
  77.8 4.0 %collective-permute-done.6 = bf16[4,2,128,128]{3,2,1,0:T(8,128)(2,1)S(1)} collective-permute-done((bf16[4,2,128,128]{3,2,1,0:T(8,128)(2,1)S(1)}, bf16[4,2,128,128]{3,2,1,0:T(8,128)(2,1)S(1)}, u32[]{:S(2)}, u32[]{:S(2)}) %collective-permute-start.6) | collective-permute-done | bytes 262176 | tf_op jit(solution)/shard_map/ppermute | solution.py:12
  81.8 0.8 constant_dynamic-update-slice_fusion.7
  82.6 0.7 constant_dynamic-update-slice_fusion.6
  83.3 6.6 %collective-permute-done.8 = bf16[4,2,128,128]{3,2,1,0:T(8,128)(2,1)S(1)} collective-permute-done((bf16[4,2,128,128]{3,2,1,0:T(8,128)(2,1)S(1)}, bf16[4,2,128,128]{3,2,1,0:T(8,128)(2,1)S(1)}, u32[]{:S(2)}, u32[]{:S(2)}) %collective-permute-start.8) | collective-permute-done | bytes 262176 | tf_op jit(solution)/shard_map/ppermute | solution.py:12
  89.9 0.7 constant_dynamic-update-slice_fusion.5
  90.7 2.4 %gather_fusion.1 = bf16[16,4,128,128]{3,2,1,0:T(8,128)(2,1)S(1)} fusion(bf16[4,14,128,128]{3,2,1,0:T(8,128)(2,1)} %constant_dynamic-update-slice_fusion.5, s32[1024]{0:T(1024)S(1)} %pad_clamp_fusion), kind=kCustom, calls=%fused_computation.1 | custom fusion | bytes 4194368 | tf_op jit(solution)/shard_map/gather | solution.py:99
  93.1 2.7 %copy.157 = bf16[2,8,4,128,128]{3,4,1,0,2:T(8,128)(2,1)} copy(bf16[2,8,4,128,128]{4,3,2,1,0:T(8,128)(2,1)S(1)} %bitcast.116) | data formatting | bytes 4194304 | tf_op jit(solution)/shard_map/gather | solution.py:99
  95.8 0.9 gather_fusion
  96.7 6.0 %multiply_reduce_fusion.3 = f32[4,2,128,128]{3,2,1,0:T(8,128)} fusion(f32[4,8]{1,0:T(4,128)S(1)} %copy.155, bf16[4,8,2,128,128]{4,3,2,1,0:T(8,128)(2,1)S(1)} %bitcast.135, bf16[4,2,2,8,128,128]{5,4,3,2,1,0:T(8,128)(2,1)} %param.8), kind=kOutput, calls=%fused_computation.7 | convolution fusion | flops 539885568 | bytes 6815872 | tf_op jit(solution)/shard_map/ijmac,ijmdc->ijmad/dot_general | solution.py:103
  102.8 6.0 %multiply_reduce_fusion.2 = f32[4,2,128,128]{3,2,1,0:T(8,128)S(1)} fusion(f32[2,8]{1,0:T(2,128)S(1)} %copy.160, bf16[2,8,4,128,128]{3,4,1,0,2:T(8,128)(2,1)} %copy.157, bf16[4,2,2,8,128,128]{5,4,3,2,1,0:T(8,128)(2,1)} %param.8), kind=kOutput, calls=%fused_computation.6 | convolution fusion | flops 539885568 | bytes 6815808 | tf_op jit(solution)/shard_map/ijmac,ijmdc->ijmad/dot_general | solution.py:109
  108.8 0.5 multiply_multiply_fusion.3
  109.7 10.8 %all_to_all.163 = f32[4,2,128,128]{3,1,0,2:T(2,128)S(1)} all-to-all(f32[4,2,128,128]{3,1,0,2:T(2,128)S(1)} %copy.161), channel_id=1, replica_groups=mesh['row'=4,'col'=8] {'col'}, dimensions={2} | all-to-all | bytes 1048576 | tf_op jit(solution)/shard_map/all_to_all | solution.py:54
  120.8 16.4 %all_to_all.164 = f32[4,16,16,128]{3,2,0,1:T(8,128)S(1)} all-to-all(f32[4,16,16,128]{3,2,0,1:T(8,128)S(1)} %copy.164), channel_id=1, replica_groups=mesh['row'=4,'col'=8] {'row'}, dimensions={1} | all-to-all | bytes 1048576 | tf_op jit(solution)/shard_map/all_to_all | solution.py:56
  137.3 12.3 %all_to_all.165 = f32[16,4,16,128]{3,2,1,0:T(8,128)S(1)} all-to-all(f32[16,4,16,128]{3,2,1,0:T(8,128)S(1)} %bitcast.125), channel_id=1, replica_groups=mesh['row'=4,'col'=8] {'col'}, dimensions={0} | all-to-all | bytes 1048576 | tf_op jit(solution)/shard_map/all_to_all | solution.py:55
  150.1 0.8 collective-permute-start.12
  150.9 2.1 collective-permute-start.13
  153.0 0.8 collective-permute-start.14
  153.8 1.5 collective-permute-start.10
  155.4 3.4 %collective-permute-done.12 = bf16[4,2,128,128]{3,2,1,0:T(8,128)(2,1)S(1)} collective-permute-done((bf16[4,2,128,128]{3,2,1,0:T(8,128)(2,1)S(1)}, bf16[4,2,128,128]{3,2,1,0:T(8,128)(2,1)S(1)}, u32[]{:S(2)}, u32[]{:S(2)}) %collective-permute-start.12) | collective-permute-done | bytes 262176 | tf_op jit(solution)/shard_map/ppermute | solution.py:12
  159.2 0.8 constant_dynamic-update-slice_fusion.23
  159.9 11.1 %collective-permute-done.9 = bf16[4,2,128,128]{3,2,1,0:T(8,128)(2,1)S(1)} collective-permute-done((bf16[4,2,128,128]{3,2,1,0:T(8,128)(2,1)S(1)}, bf16[4,2,128,128]{3,2,1,0:T(8,128)(2,1)S(1)}, u32[]{:S(2)}, u32[]{:S(2)}) %collective-permute-start.9) | collective-permute-done | bytes 262176 | tf_op jit(solution)/shard_map/ppermute | solution.py:12
  171.0 0.5 collective-permute-start.15
  171.6 1.2 collective-permute-start.16
  172.8 0.8 constant_dynamic-update-slice_fusion.22
  173.5 1.9 collective-permute-start.17
  175.4 0.8 constant_dynamic-update-slice_fusion.21
  176.2 0.8 constant_dynamic-update-slice_fusion.20
  177.2 2.1 gather_fusion.2
  179.4 6.6 %multiply_reduce_fusion.1 = f32[4,2,128,128]{3,2,1,0:T(8,128)} fusion(bf16[4,8,2,128,128]{4,3,2,1,0:T(8,128)(2,1)} %bitcast.134, f32[4,8]{1,0:T(4,128)S(1)} %copy.155, bf16[4,2,2,8,128,128]{5,4,3,2,1,0:T(8,128)(2,1)} %param.8), kind=kOutput, calls=%fused_computation.5 | convolution fusion | flops 539885568 | bytes 6815872 | tf_op jit(solution)/shard_map/ijmac,ijmdc->ijmad/dot_general | solution.py:103
  186.0 0.7 constant_dynamic-update-slice_fusion.19
  186.7 0.7 constant_dynamic-update-slice_fusion.18
  187.5 1.5 collective-permute-done.17
  189.0 0.7 constant_dynamic-update-slice_fusion.17
  189.7 2.4 %gather_fusion.3 = bf16[16,4,128,128]{3,2,1,0:T(8,128)(2,1)S(1)} fusion(bf16[4,14,128,128]{3,2,1,0:T(8,128)(2,1)} %constant_dynamic-update-slice_fusion.17, s32[1024]{0:T(1024)S(1)} %pad_clamp_fusion), kind=kCustom, calls=%fused_computation.3 | custom fusion | bytes 4194368 | tf_op jit(solution)/shard_map/gather | solution.py:99
  192.2 2.7 %copy.171 = bf16[2,8,4,128,128]{3,4,1,0,2:T(8,128)(2,1)} copy(bf16[2,8,4,128,128]{4,3,2,1,0:T(8,128)(2,1)S(1)} %bitcast.115) | data formatting | bytes 4194304 | tf_op jit(solution)/shard_map/gather | solution.py:99
  194.8 6.0 %multiply_reduce_fusion = f32[4,2,128,128]{3,2,1,0:T(8,128)S(1)} fusion(bf16[2,8,4,128,128]{3,4,1,0,2:T(8,128)(2,1)} %copy.171, f32[2,8]{1,0:T(2,128)S(1)} %copy.160, bf16[4,2,2,8,128,128]{5,4,3,2,1,0:T(8,128)(2,1)} %param.8), kind=kOutput, calls=%fused_computation.4 | convolution fusion | flops 539885568 | bytes 6815808 | tf_op jit(solution)/shard_map/ijmac,ijmdc->ijmad/dot_general | solution.py:109
  200.8 1.1 multiply_multiply_fusion.1
  202.4 11.7 %all_to_all.166 = f32[4,2,128,128]{3,1,0,2:T(2,128)S(1)} all-to-all(f32[4,2,128,128]{3,1,0,2:T(2,128)S(1)} %copy.173), channel_id=1, replica_groups=mesh['row'=4,'col'=8] {'col'}, dimensions={2} | all-to-all | bytes 1048576 | tf_op jit(solution)/shard_map/all_to_all | solution.py:54
  214.3 16.4 %all_to_all.167 = f32[4,16,16,128]{3,2,0,1:T(8,128)S(1)} all-to-all(f32[4,16,16,128]{3,2,0,1:T(8,128)S(1)} %copy.176), channel_id=1, replica_groups=mesh['row'=4,'col'=8] {'row'}, dimensions={1} | all-to-all | bytes 1048576 | tf_op jit(solution)/shard_map/all_to_all | solution.py:56
  230.8 12.3 %all_to_all.168 = f32[16,4,16,128]{3,2,1,0:T(8,128)S(1)} all-to-all(f32[16,4,16,128]{3,2,1,0:T(8,128)S(1)} %bitcast.131), channel_id=1, replica_groups=mesh['row'=4,'col'=8] {'col'}, dimensions={0} | all-to-all | bytes 1048576 | tf_op jit(solution)/shard_map/all_to_all | solution.py:55
  243.4 1.0 multiply_multiply_fusion
  (80 shorter events, 5.4 us)
Async XLA Ops:
  0.6 22.1 %copy-start = (f32[16,8]{0,1:T(8,128)S(1)}, f32[16,8]{0,1:T(8,128)}, u32[]{:S(2)}) copy-start(f32[16,8]{0,1:T(8,128)} %param.12) | copy-start | bytes 1540
  17.3 25.6 %copy-start.8 = (s32[16,8]{0,1:T(8,128)S(1)}, s32[16,8]{0,1:T(8,128)}, u32[]{:S(2)}) copy-start(s32[16,8]{0,1:T(8,128)} %param.13) | copy-start | bytes 1540
  18.2 18.6 %all-to-all-start.1 = ((f32[4,16,16,128]{3,2,0,1:T(8,128)}), f32[4,16,16,128]{3,2,0,1:T(8,128)S(1)}, u32[]{:S(2)}, u32[]{:S(2)}) async-start(f32[4,16,16,128]{3,2,0,1:T(8,128)} %copy.146), calls=%async_computation.1 | async-start | bytes 1048576 | tf_op jit(solution)/shard_map/all_to_all | solution.py:56
  36.8 14.6 %copy-start.1 = (f32[4,2,128,128]{3,2,1,0:T(8,128)S(1)}, f32[4,2,128,128]{3,2,1,0:T(8,128)}, u32[]{:S(2)}) copy-start(f32[4,2,128,128]{3,2,1,0:T(8,128)} %param.7) | copy-start | bytes 1572868
  36.8 14.6 %copy-start.7 = (f32[4,2,128]{2,1,0:T(2,128)S(1)}, f32[4,2,128]{2,1,0:T(2,128)}, u32[]{:S(2)}) copy-start(f32[4,2,128]{2,1,0:T(2,128)} %param.9) | copy-start | bytes 12292
  37.7 13.5 %all-to-all-start.2 = ((f32[16,4,16,128]{3,2,1,0:T(8,128)}), f32[16,4,16,128]{3,2,1,0:T(8,128)S(1)}, u32[]{:S(2)}, u32[]{:S(2)}) async-start(f32[16,4,16,128]{3,2,1,0:T(8,128)} %bitcast.6), calls=%async_computation.2 | async-start | bytes 1048576 | tf_op jit(solution)/shard_map/all_to_all | solution.py:55
  51.4 26.2 %copy-start.3 = (f32[2,4,128,128]{2,3,0,1:T(8,128)}, f32[2,4,128,128]{2,3,0,1:T(8,128)S(1)}, u32[]{:S(2)}) copy-start(f32[2,4,128,128]{2,3,0,1:T(8,128)S(1)} %copy.150) | copy-start | bytes 1572868
  51.8 8.5 %collective-permute-start.3 = (bf16[4,2,128,128]{3,2,1,0:T(8,128)(2,1)S(1)}, bf16[4,2,128,128]{3,2,1,0:T(8,128)(2,1)S(1)}, u32[]{:S(2)}, u32[]{:S(2)}) collective-permute-start(bf16[4,2,128,128]{3,2,1,0:T(8,128)(2,1)S(1)} %fusion.63), channel_id=1, source_target_pairs={{0,3},{1,4},{2,5},{3,6},{4,7},{5,0},{6,1},{7,2},{8,11},{9,12},{10,... | collective-permute-start | bytes 786440 | tf_op jit(solution)/shard_map/ppermute | solution.py:12
  52.7 19.3 %collective-permute-start = (bf16[4,2,128,128]{3,2,1,0:T(8,128)(2,1)S(1)}, bf16[4,2,128,128]{3,2,1,0:T(8,128)(2,1)S(1)}, u32[]{:S(2)}, u32[]{:S(2)}) collective-permute-start(bf16[4,2,128,128]{3,2,1,0:T(8,128)(2,1)S(1)} %fusion.63), channel_id=1, source_target_pairs={{0,16},{8,24},{16,0},{24,8},{1,17},{9,25},{17,1},{25,9},{2,18},{10... | collective-permute-start | bytes 786440 | tf_op jit(solution)/shard_map/ppermute | solution.py:12
  52.9 19.6 %collective-permute-start.4 = (bf16[4,2,128,128]{3,2,1,0:T(8,128)(2,1)S(1)}, bf16[4,2,128,128]{3,2,1,0:T(8,128)(2,1)S(1)}, u32[]{:S(2)}, u32[]{:S(2)}) collective-permute-start(bf16[4,2,128,128]{3,2,1,0:T(8,128)(2,1)S(1)} %fusion.63), channel_id=1, source_target_pairs={{0,2},{1,3},{2,4},{3,5},{4,6},{5,7},{6,0},{7,1},{8,10},{9,11},{10,... | collective-permute-start | bytes 786440 | tf_op jit(solution)/shard_map/ppermute | solution.py:12
  55.1 19.3 %collective-permute-start.5 = (bf16[4,2,128,128]{3,2,1,0:T(8,128)(2,1)S(1)}, bf16[4,2,128,128]{3,2,1,0:T(8,128)(2,1)S(1)}, u32[]{:S(2)}, u32[]{:S(2)}) collective-permute-start(bf16[4,2,128,128]{3,2,1,0:T(8,128)(2,1)S(1)} %fusion.63), channel_id=1, source_target_pairs={{0,1},{1,2},{2,3},{3,4},{4,5},{5,6},{6,7},{7,0},{8,9},{9,10},{10,1... | collective-permute-start | bytes 786440 | tf_op jit(solution)/shard_map/ppermute | solution.py:12
  55.1 21.7 %collective-permute-start.1 = (bf16[4,2,128,128]{3,2,1,0:T(8,128)(2,1)S(1)}, bf16[4,2,128,128]{3,2,1,0:T(8,128)(2,1)S(1)}, u32[]{:S(2)}, u32[]{:S(2)}) collective-permute-start(bf16[4,2,128,128]{3,2,1,0:T(8,128)(2,1)S(1)} %fusion.63), channel_id=1, source_target_pairs={{0,8},{8,16},{16,24},{24,0},{1,9},{9,17},{17,25},{25,1},{2,10},{10... | collective-permute-start | bytes 786440 | tf_op jit(solution)/shard_map/ppermute | solution.py:12
  60.3 17.4 %collective-permute-start.2 = (bf16[4,2,128,128]{3,2,1,0:T(8,128)(2,1)S(1)}, bf16[4,2,128,128]{3,2,1,0:T(8,128)(2,1)S(1)}, u32[]{:S(2)}, u32[]{:S(2)}) collective-permute-start(bf16[4,2,128,128]{3,2,1,0:T(8,128)(2,1)S(1)} %fusion.63), channel_id=1, source_target_pairs={{0,24},{8,0},{16,8},{24,16},{1,25},{9,1},{17,9},{25,17},{2,26},{10... | collective-permute-start | bytes 786440 | tf_op jit(solution)/shard_map/ppermute | solution.py:12
  72.0 9.8 %collective-permute-start.6 = (bf16[4,2,128,128]{3,2,1,0:T(8,128)(2,1)S(1)}, bf16[4,2,128,128]{3,2,1,0:T(8,128)(2,1)S(1)}, u32[]{:S(2)}, u32[]{:S(2)}) collective-permute-start(bf16[4,2,128,128]{3,2,1,0:T(8,128)(2,1)S(1)} %fusion.63), channel_id=1, source_target_pairs={{0,7},{1,0},{2,1},{3,2},{4,3},{5,4},{6,5},{7,6},{8,15},{9,8},{10,9... | collective-permute-start | bytes 786440 | tf_op jit(solution)/shard_map/ppermute | solution.py:12
  72.5 10.1 %collective-permute-start.7 = (bf16[4,2,128,128]{3,2,1,0:T(8,128)(2,1)S(1)}, bf16[4,2,128,128]{3,2,1,0:T(8,128)(2,1)S(1)}, u32[]{:S(2)}, u32[]{:S(2)}) collective-permute-start(bf16[4,2,128,128]{3,2,1,0:T(8,128)(2,1)S(1)} %fusion.63), channel_id=1, source_target_pairs={{0,6},{1,7},{2,0},{3,1},{4,2},{5,3},{6,4},{7,5},{8,14},{9,15},{10,... | collective-permute-start | bytes 786440 | tf_op jit(solution)/shard_map/ppermute | solution.py:12
  74.5 15.4 %collective-permute-start.8 = (bf16[4,2,128,128]{3,2,1,0:T(8,128)(2,1)S(1)}, bf16[4,2,128,128]{3,2,1,0:T(8,128)(2,1)S(1)}, u32[]{:S(2)}, u32[]{:S(2)}) collective-permute-start(bf16[4,2,128,128]{3,2,1,0:T(8,128)(2,1)S(1)} %fusion.63), channel_id=1, source_target_pairs={{0,5},{1,6},{2,7},{3,0},{4,1},{5,2},{6,3},{7,4},{8,13},{9,14},{10,... | collective-permute-start | bytes 786440 | tf_op jit(solution)/shard_map/ppermute | solution.py:12
  102.8 6.0 %copy-start.2 = (f32[4,2,128,128]{3,2,1,0:T(8,128)S(1)}, f32[4,2,128,128]{3,2,1,0:T(8,128)}, u32[]{:S(2)}) copy-start(f32[4,2,128,128]{3,2,1,0:T(8,128)} %param.7) | copy-start | bytes 1572868
  102.8 6.0 %copy-start.4 = (f32[2,4,128,128]{2,3,0,1:T(8,128)S(1)}, f32[2,4,128,128]{2,3,0,1:T(8,128)}, u32[]{:S(2)}) copy-start(f32[2,4,128,128]{2,3,0,1:T(8,128)} %copy-done.3) | copy-start | bytes 1572868
  102.8 6.1 %copy-start.5 = (f32[4,2,128,128]{3,2,1,0:T(8,128)S(1)}, f32[4,2,128,128]{3,2,1,0:T(8,128)}, u32[]{:S(2)}) copy-start(f32[4,2,128,128]{3,2,1,0:T(8,128)} %multiply_reduce_fusion.3) | copy-start | bytes 1572868
  150.1 8.7 %collective-permute-start.12 = (bf16[4,2,128,128]{3,2,1,0:T(8,128)(2,1)S(1)}, bf16[4,2,128,128]{3,2,1,0:T(8,128)(2,1)S(1)}, u32[]{:S(2)}, u32[]{:S(2)}) collective-permute-start(bf16[4,2,128,128]{3,2,1,0:T(8,128)(2,1)S(1)} %get-tuple-element.10), channel_id=1, source_target_pairs={{0,3},{1,4},{2,5},{3,6},{4,7},{5,0},{6,1},{7,2},{8,11},{9,12},{10,... | collective-permute-start | bytes 786440 | tf_op jit(solution)/shard_map/ppermute | solution.py:12
  150.9 20.1 %collective-permute-start.9 = (bf16[4,2,128,128]{3,2,1,0:T(8,128)(2,1)S(1)}, bf16[4,2,128,128]{3,2,1,0:T(8,128)(2,1)S(1)}, u32[]{:S(2)}, u32[]{:S(2)}) collective-permute-start(bf16[4,2,128,128]{3,2,1,0:T(8,128)(2,1)S(1)} %get-tuple-element.10), channel_id=1, source_target_pairs={{0,16},{8,24},{16,0},{24,8},{1,17},{9,25},{17,1},{25,9},{2,18},{10... | collective-permute-start | bytes 786440 | tf_op jit(solution)/shard_map/ppermute | solution.py:12
  150.9 20.6 %collective-permute-start.13 = (bf16[4,2,128,128]{3,2,1,0:T(8,128)(2,1)S(1)}, bf16[4,2,128,128]{3,2,1,0:T(8,128)(2,1)S(1)}, u32[]{:S(2)}, u32[]{:S(2)}) collective-permute-start(bf16[4,2,128,128]{3,2,1,0:T(8,128)(2,1)S(1)} %get-tuple-element.10), channel_id=1, source_target_pairs={{0,2},{1,3},{2,4},{3,5},{4,6},{5,7},{6,0},{7,1},{8,10},{9,11},{10,... | collective-permute-start | bytes 786440 | tf_op jit(solution)/shard_map/ppermute | solution.py:12
  153.0 20.5 %collective-permute-start.14 = (bf16[4,2,128,128]{3,2,1,0:T(8,128)(2,1)S(1)}, bf16[4,2,128,128]{3,2,1,0:T(8,128)(2,1)S(1)}, u32[]{:S(2)}, u32[]{:S(2)}) collective-permute-start(bf16[4,2,128,128]{3,2,1,0:T(8,128)(2,1)S(1)} %get-tuple-element.10), channel_id=1, source_target_pairs={{0,1},{1,2},{2,3},{3,4},{4,5},{5,6},{6,7},{7,0},{8,9},{9,10},{10,1... | collective-permute-start | bytes 786440 | tf_op jit(solution)/shard_map/ppermute | solution.py:12
  153.8 22.4 %collective-permute-start.10 = (bf16[4,2,128,128]{3,2,1,0:T(8,128)(2,1)S(1)}, bf16[4,2,128,128]{3,2,1,0:T(8,128)(2,1)S(1)}, u32[]{:S(2)}, u32[]{:S(2)}) collective-permute-start(bf16[4,2,128,128]{3,2,1,0:T(8,128)(2,1)S(1)} %get-tuple-element.10), channel_id=1, source_target_pairs={{0,8},{8,16},{16,24},{24,0},{1,9},{9,17},{17,25},{25,1},{2,10},{10... | collective-permute-start | bytes 786440 | tf_op jit(solution)/shard_map/ppermute | solution.py:12
  158.8 18.2 %collective-permute-start.11 = (bf16[4,2,128,128]{3,2,1,0:T(8,128)(2,1)S(1)}, bf16[4,2,128,128]{3,2,1,0:T(8,128)(2,1)S(1)}, u32[]{:S(2)}, u32[]{:S(2)}) collective-permute-start(bf16[4,2,128,128]{3,2,1,0:T(8,128)(2,1)S(1)} %get-tuple-element.10), channel_id=1, source_target_pairs={{0,24},{8,0},{16,8},{24,16},{1,25},{9,1},{17,9},{25,17},{2,26},{10... | collective-permute-start | bytes 786440 | tf_op jit(solution)/shard_map/ppermute | solution.py:12
  171.0 15.0 %collective-permute-start.15 = (bf16[4,2,128,128]{3,2,1,0:T(8,128)(2,1)S(1)}, bf16[4,2,128,128]{3,2,1,0:T(8,128)(2,1)S(1)}, u32[]{:S(2)}, u32[]{:S(2)}) collective-permute-start(bf16[4,2,128,128]{3,2,1,0:T(8,128)(2,1)S(1)} %get-tuple-element.10), channel_id=1, source_target_pairs={{0,7},{1,0},{2,1},{3,2},{4,3},{5,4},{6,5},{7,6},{8,15},{9,8},{10,9... | collective-permute-start | bytes 786440 | tf_op jit(solution)/shard_map/ppermute | solution.py:12
  171.6 15.2 %collective-permute-start.16 = (bf16[4,2,128,128]{3,2,1,0:T(8,128)(2,1)S(1)}, bf16[4,2,128,128]{3,2,1,0:T(8,128)(2,1)S(1)}, u32[]{:S(2)}, u32[]{:S(2)}) collective-permute-start(bf16[4,2,128,128]{3,2,1,0:T(8,128)(2,1)S(1)} %get-tuple-element.10), channel_id=1, source_target_pairs={{0,6},{1,7},{2,0},{3,1},{4,2},{5,3},{6,4},{7,5},{8,14},{9,15},{10,... | collective-permute-start | bytes 786440 | tf_op jit(solution)/shard_map/ppermute | solution.py:12
  173.5 15.4 %collective-permute-start.17 = (bf16[4,2,128,128]{3,2,1,0:T(8,128)(2,1)S(1)}, bf16[4,2,128,128]{3,2,1,0:T(8,128)(2,1)S(1)}, u32[]{:S(2)}, u32[]{:S(2)}) collective-permute-start(bf16[4,2,128,128]{3,2,1,0:T(8,128)(2,1)S(1)} %get-tuple-element.10), channel_id=1, source_target_pairs={{0,5},{1,6},{2,7},{3,0},{4,1},{5,2},{6,3},{7,4},{8,13},{9,14},{10,... | collective-permute-start | bytes 786440 | tf_op jit(solution)/shard_map/ppermute | solution.py:12
  194.8 6.0 %copy-start.6 = (f32[4,2,128,128]{3,2,1,0:T(8,128)S(1)}, f32[4,2,128,128]{3,2,1,0:T(8,128)}, u32[]{:S(2)}) copy-start(f32[4,2,128,128]{3,2,1,0:T(8,128)} %multiply_reduce_fusion.1) | copy-start | bytes 1572868
where the time goes:
time: 247 us; the launch traced here: 244 us
  blocking collectives  92.4 us (37%)
  waiting for transfers between devices  62.1 us (25%)
  local copies, waits for them, and re-layouts  31.5 us (13%)
  starting transfers between devices  27.8 us (11%)
  matrix products  24.6 us (10%)
  other arithmetic  4.85 us (2%)
    ppermute x18, waiting for transfers between devices, from_behind(): lax.ppermute(value, axis, [(i, (i + by) % peers) for i in range(peers)])  40.1 us
    all_to_all x3, blocking collectives, mirror(): lax.all_to_all(updated, 'col', split_axis=2, concat_axis=1, tiled=True)  35 us
    all_to_all x2, blocking collectives, mirror(): lax.all_to_all(spread, 'row', split_axis=1, concat_axis=0, tiled=True)  32.9 us
    all_to_all x2, blocking collectives, mirror(): lax.all_to_all(lax.all_to_all(spread, 'row', split_axis=1, concat_axis=0,...  24.6 us
    ppermute x18, starting transfers between devices, from_behind(): lax.ppermute(value, axis, [(i, (i + by) % peers) for i in range(peers)])  18 us
    all_to_all x1, waiting for transfers between devices, mirror(): lax.all_to_all(spread, 'row', split_axis=1, concat_axis=0, tiled=True)  14 us
    dot_general x2, matrix products, per_device(): jnp.einsum('ijmac,ijmdc->ijmad', half_rows, side_rows, preferred_element_...  12.7 us
    dot_general x2, matrix products, per_device(): jnp.einsum('ijmac,ijmdc->ijmad', half_cols, side_cols, preferred_element_...  12 us
  transfers between devices with their start and end apart: 20, of which 9 were waited for; matrix products, arithmetic and copies ran while one was open for 8% of the time, Pallas kernels for 0%

commit v1 on v0

v1 whole, which is shorter than its diff:
```python
import functools

import jax
import jax.numpy as jnp
from jax import lax
from jax.experimental import pallas as pl
from jax.experimental.pallas import tpu as pltpu
from jax.sharding import PartitionSpec as P

REACH = 6
ITERS = 3
MESH = pl.DeviceIdType.MESH
BF16 = jnp.bfloat16
F32 = jnp.float32


def spread(amount, peers):
    shards = -(-REACH // amount)
    whole = 2 * shards + 2 >= peers
    steps = [d for d in range(-shards, shards + 1) if d]
    if whole:
        steps = sorted({d % peers for d in steps})
    return whole, shards, steps


def flip(value, bit):
    return value + bit - 2 * bit * ((value // bit) % 2)


class Side:
    def __init__(self, amount, peers, me):
        self.amount, self.peers, self.me = amount, peers, me
        self.whole, self.shards, self.steps = spread(amount, peers)

    def slots(self):
        return (self.peers if self.whole else 2 * self.shards + 1) * self.amount

    def place(self, k):
        if self.whole:
            return k
        shard = lax.rem(k // self.amount - self.me + self.shards + self.peers, self.peers)
        return shard * self.amount + lax.rem(k, self.amount)

    def block(self, owner):
        return pl.ds(owner * self.amount, self.amount)

    def own(self):
        return self.me if self.whole else self.shards

    def landing(self, step):
        return self.me if self.whole else self.shards - step


def kernel(sizes, exch, marg_hbm, energy, count, occ, coupling, nbr, amp_out, res_out, *scratch):
    nr, nc, rows, cols, width, listed = sizes
    q = nr // nc
    sweeps = ITERS - 1
    scratch = list(scratch)
    marg, weight, denom, both, amps, coup, sent, mirrored = scratch[:8]
    del scratch[:8]
    row_bufs = [[scratch.pop(0) for _ in range(nc)] for _ in range(sweeps)]
    col_bufs = [[scratch.pop(0) for _ in range(nr)] for _ in range(sweeps)]
    marg_sem, mir_send, mir_recv, row_send, row_recv, col_send, col_recv = scratch

    r = lax.axis_index("row")
    c = lax.axis_index("col")
    rside, cside = Side(nr, rows, r), Side(nc, cols, c)
    ring = rside.whole and rows == 4 and nc % 2 == 0
    cube = cside.whole and cols == 8

    load = pltpu.make_async_copy(marg_hbm, marg, marg_sem)
    load.start()

    on_diagonal = c // q == r
    def partner(p):
        return (c // q, r * q + p)
    def is_self(p):
        return jnp.logical_and(on_diagonal, lax.rem(c, q) == p)
    def shift(step):
        return lax.rem(r + step + rows, rows)

    row_peers = [1, rows - 1] if ring else rside.steps
    if cube:
        col_peers = [flip(c, 1), flip(c, 2), flip(c, 4)]
    else:
        col_peers = [lax.rem(c + d + cols, cols) for d in cside.steps]
    barrier = pltpu.get_barrier_semaphore()
    for d in row_peers:
        pl.semaphore_signal(barrier, inc=1, device_id=(shift(d), c), device_id_type=MESH)
    for peer in col_peers:
        pl.semaphore_signal(barrier, inc=1, device_id=(r, peer), device_id_type=MESH)
    for p in range(q):
        @pl.when(jnp.logical_not(is_self(p)))
        def _():
            pl.semaphore_signal(barrier, inc=1, device_id=partner(p), device_id_type=MESH)

    def remote(src, dst, ssem, rsem, where):
        return pltpu.make_async_remote_copy(
            src_ref=src, dst_ref=dst, send_sem=ssem, recv_sem=rsem, device_id=where, device_id_type=MESH)

    def mirror_copy(phase, p, b):
        return remote(
            sent.at[phase, p, b], mirrored.at[phase, lax.rem(c, q), b],
            mir_send.at[phase, p, b], mir_recv.at[phase, lax.rem(c, q), b], partner(p))

    def mirror_arrival(phase, p, b):
        return remote(
            sent.at[phase, p, b], mirrored.at[phase, p, b],
            mir_send.at[phase, p, b], mir_recv.at[phase, p, b], partner(p))

    def mirror_start(phase, b):
        for p in range(q):
            @pl.when(jnp.logical_not(is_self(p)))
            def _():
                mirror_copy(phase, p, b).start()

            @pl.when(is_self(p))
            def _():
                mirrored[phase, p, b] = sent[phase, p, b]

    def mirror_wait(phase, b):
        for p in range(q):
            @pl.when(jnp.logical_not(is_self(p)))
            def _():
                mirror_arrival(phase, p, b).wait_recv()
                mirror_copy(phase, p, b).wait_send()

    line = lax.broadcasted_iota(jnp.int32, (width, width), 0)
    lane = lax.broadcasted_iota(jnp.int32, (width, width), 1)

    def prepare(i, b):
        e = jnp.broadcast_to(energy[i, pl.ds(b, 1), :], (width, width))
        d = e.T + e - occ[r * nr + i] - occ[c * nc + b]
        live = jnp.logical_and(line < count[i, b], lane < count[i, b])
        w = jnp.where(live, 1.0 / d, 0.0)
        g = exch[i, b] * w
        high = g.astype(BF16)
        weight[i, b] = w
        denom[i, b] = d
        both[i, b] = g
        coup[i, b] = jnp.zeros((width, width), F32)
        sent[0, i // nc, b, lax.rem(i, nc)] = high
        sent[1, i // nc, b, lax.rem(i, nc)] = (g - high.astype(F32)).astype(BF16)

    for b in range(nc):
        def body(i, carry):
            prepare(i, b)
            return carry
        lax.fori_loop(0, nr, body, 0)

    amount = len(row_peers) + len(col_peers) + q
    @pl.when(on_diagonal)
    def _():
        pl.semaphore_wait(barrier, amount - 1)
    @pl.when(jnp.logical_not(on_diagonal))
    def _():
        pl.semaphore_wait(barrier, amount)

    for phase in range(2):
        for b in range(nc):
            mirror_start(phase, b)

    def reflection(phase, i, j):
        return mirrored[phase, i // nc, lax.rem(i, nc), j].astype(F32).T

    def row_copy(s, j, which):
        buf = row_bufs[s][j]
        def one(owner, landing, step):
            return remote(buf.at[rside.block(owner)], buf.at[rside.block(landing)],
                          row_send.at[s, j, which], row_recv.at[s, j, which], (shift(step), c))
        if ring:
            if which == 0:
                return one(r, r, 1)
            if which == 1:
                return one(r, r, rows - 1)
            return one(shift(-1), shift(-1), 1) if j < nc // 2 else one(shift(1), shift(1), rows - 1)
        step = rside.steps[which]
        return one(rside.own(), rside.landing(step), step)

    def col_copy(s, i, which):
        buf = col_bufs[s][i]
        def one(owner, landing, peer):
            return remote(buf.at[cside.block(owner)], buf.at[cside.block(landing)],
                          col_send.at[s, i, which], col_recv.at[s, i, which], (r, peer))
        if cube:
            near, side, across = flip(c, 1), flip(c, 2), flip(c, 4)
            if which == 0:
                return one(c, c, side)
            if which == 1:
                return one(c, c, across)
            if which == 2:
                return one(side, side, across) if i < nr // 2 else one(across, across, side)
            block = (c, side, across, flip(side, 4))[which - 3]
            return one(block, block, near)
        step = cside.steps[which]
        return one(cside.own(), cside.landing(step), lax.rem(c + step + cols, cols))

    def col_first(s, i):
        for w in ((0, 1, 3) if cube else range(len(cside.steps))):
            col_copy(s, i, w).start()

    def row_first(s, j):
        for w in range(2 if ring else len(rside.steps)):
            row_copy(s, j, w).start()

    def col_second(s, i):
        if cube:
            for w in (0, 1):
                col_copy(s, i, w).wait_recv()
            for w in (2, 4, 5):
                col_copy(s, i, w).start()

    def col_third(s, i):
        if cube:
            col_copy(s, i, 2).wait_recv()
            col_copy(s, i, 6).start()

    def col_last(s, i):
        for w in (range(3, 7) if cube else range(len(cside.steps))):
            col_copy(s, i, w).wait_recv()

    def row_second(s, j):
        if ring:
            for w in (0, 1):
                row_copy(s, j, w).wait_recv()
            row_copy(s, j, 2).start()

    def row_last(s, j):
        for w in ((2,) if ring else range(len(rside.steps))):
            row_copy(s, j, w).wait_recv()

    def two_sided(buf, side, i, j, owner, place):
        halves, sides = [], []
        for m in range(listed):
            block = buf[place(nbr[owner, m])]
            s = marg[i, j, side, m]
            half = jnp.dot(s, block, preferred_element_type=F32) * coupling[owner, m]
            halves.append(half.astype(BF16))
            sides.append(s)
        full = lax.dot_general(
            jnp.concatenate(halves, axis=1), jnp.concatenate(sides, axis=1),
            (((1,), (1,)), ((), ())), preferred_element_type=F32)
        coup[i, j] = coup[i, j] + full

    def col_products(s, i):
        def body(j, carry):
            two_sided(col_bufs[s][i], 1, i, j, c * nc + j, cside.place)
            return carry
        lax.fori_loop(0, nc, body, 0)

    def row_products(s, j):
        def body(i, carry):
            two_sided(row_bufs[s][j], 0, i, j, r * nr + i, rside.place)
            return carry
        lax.fori_loop(0, nr, body, 0)

    def own_slot(side, local):
        return side.own() * side.amount + local

    for s in range(sweeps):
        for b in range(nc):
            mirror_wait(0 if s == 0 else s + 1, b)
        for i in range(nr):
            for j in range(nc):
                if s == 0:
                    total = both[i, j] + reflection(0, i, j)
                    amp = jnp.where(weight[i, j] != 0.0, -0.5 * total, 0.0)
                else:
                    total = coup[i, j] * weight[i, j] + reflection(s + 1, i, j) - both[i, j]
                    amp = jnp.where(weight[i, j] != 0.0, 0.5 * total, 0.0)
                    coup[i, j] = jnp.zeros((width, width), F32)
                if s == sweeps - 1:
                    amps[i, j] = amp
                small = amp.astype(BF16)
                row_bufs[s][j][own_slot(rside, i)] = small
                col_bufs[s][i][own_slot(cside, j)] = small
            col_first(s, i)
        for j in range(nc):
            row_first(s, j)
        if s == 0:
            load.wait()
            for b in range(nc):
                mirror_wait(1, b)
            for i in range(nr):
                for j in range(nc):
                    both[i, j] = both[i, j] + (reflection(0, i, j) + reflection(1, i, j))
        for t in range(nr + 2):
            if t < nr:
                col_second(s, t)
            if t < nc:
                row_second(s, t)
            if 1 <= t <= nr:
                col_third(s, t - 1)
            if t >= 2:
                col_last(s, t - 2)
                col_products(s, t - 2)
        for j in range(nc):
            row_last(s, j)
            row_products(s, j)
            for i in range(nr):
                sent[s + 2, i // nc, j, i % nc] = (coup[i, j] * weight[i, j]).astype(BF16)
            mirror_start(s + 2, j)

    for i in range(nr):
        for j in range(nc):
            res_out[i, j] = exch[i, j] + denom[i, j] * amps[i, j] - coup[i, j]
    for s in range(sweeps):
        for i in range(nr):
            for w in range(7 if cube else len(cside.steps)):
                col_copy(s, i, w).wait_send()
        for j in range(nc):
            for w in range(3 if ring else len(rside.steps)):
                row_copy(s, j, w).wait_send()
    for b in range(nc):
        mirror_wait(sweeps + 1, b)
    for i in range(nr):
        for j in range(nc):
            total = coup[i, j] * weight[i, j] + reflection(sweeps + 1, i, j) - both[i, j]
            amp_out[i, j] = jnp.where(weight[i, j] != 0.0, 0.5 * total, 0.0)


def per_device(rows, cols, exch, margins, energy, count, occ, coupling, nbr):
    nr, nc, width, _ = exch.shape
    listed = nbr.shape[1]
    sweeps = ITERS - 1
    q = nr // nc
    rside, cside = Side(nr, rows, 0), Side(nc, cols, 0)
    pairs = pltpu.VMEM((nr, nc, width, width), F32)
    mirror = pltpu.VMEM((sweeps + 2, q, nc, nc, width, width), BF16)
    dma = pltpu.SemaphoreType.DMA
    rsteps, csteps = max(3, len(rside.steps)), max(7, len(cside.steps))
    scratch = [pltpu.VMEM(margins.shape, BF16)] + [pairs] * 5 + [mirror] * 2
    scratch += [pltpu.VMEM((rside.slots(), width, width), BF16)] * (sweeps * nc)
    scratch += [pltpu.VMEM((cside.slots(), width, width), BF16)] * (sweeps * nr)
    scratch += [dma, dma((sweeps + 2, q, nc)), dma((sweeps + 2, q, nc))]
    scratch += [dma((sweeps, nc, rsteps))] * 2 + [dma((sweeps, nr, csteps))] * 2
    vmem = pl.BlockSpec(memory_space=pltpu.VMEM)
    smem = pl.BlockSpec(memory_space=pltpu.SMEM)
    return pl.pallas_call(
        functools.partial(kernel, (nr, nc, rows, cols, width, listed)),
        out_shape=(jax.ShapeDtypeStruct(exch.shape, F32), jax.ShapeDtypeStruct(exch.shape, F32)),
        in_specs=[vmem, pl.BlockSpec(memory_space=pl.ANY), vmem, smem, smem, smem, smem],
        out_specs=(vmem, vmem),
        scratch_shapes=scratch,
        compiler_params=pltpu.CompilerParams(
            collective_id=0, has_side_effects=True, vmem_limit_bytes=56 * 2**20),
        name="sweeps",
    )(exch, margins, energy, count, occ, coupling, nbr)


def solution(mesh):
    return jax.shard_map(
        functools.partial(per_device, mesh.shape["row"], mesh.shape["col"]),
        mesh=mesh,
        in_specs=(
            P("row", "col", None, None),
            P("row", "col", None, None, None, None),
            P("row", "col", None),
            P("row", "col"),
            P(),
            P(),
            P(),
        ),
        out_specs=(P("row", "col", None, None), P("row", "col", None, None)),
        check_vma=False,
    )
```

time: 247 us -> 131 us (0.53)
  Pallas kernels: 0 us -> 122 us
  blocking collectives: 92.4 us -> 0 us
  waiting for transfers between devices: 62.1 us -> 0 us
  starting transfers between devices: 27.8 us -> 0 us
  matrix products: 24.6 us -> 0 us
  local copies, waits for them, and re-layouts: 31.5 us -> 7.8 us
  other arithmetic: 4.85 us -> 0 us
    pallas_call x0 -> x1, Pallas kernels: none -> 122 us  [per_device(): pl.pallas_call(functools.partial(kernel, (nr, nc, rows, cols, width, list...]
    all_to_all x7 -> x0, blocking collectives: 92.4 us -> none  [the longest x3 35 us: mirror(): lax.all_to_all(updated, 'col', split_axis=2, concat_axis=1, tiled=True)]
    ppermute x18 -> x0, waiting for transfers between devices: 40.1 us -> none  [from_behind(): lax.ppermute(value, axis, [(i, (i + by) % peers) for i in range(peers)])]
    dot_general x4 -> x0, matrix products: 24.6 us -> none  [the longest x2 12.7 us: per_device(): jnp.einsum('ijmac,ijmdc->ijmad', half_rows, side_rows, preferred_element_...]
    all_to_all x2 -> x0, waiting for transfers between devices: 22 us -> none  [the longest x1 14 us: mirror(): lax.all_to_all(spread, 'row', split_axis=1, concat_axis=0, tiled=True)]
    ppermute x18 -> x0, starting transfers between devices: 18 us -> none  [from_behind(): lax.ppermute(value, axis, [(i, (i + by) % peers) for i in range(peers)])]
    gather x6 -> x0, local copies, waits for them, and re-layouts: 13.3 us -> none  [the longest x4 10.2 us: per_device(): near_cols = cols_wide[:, place_cols]]
    all_to_all x2 -> x0, starting transfers between devices: 9.85 us -> none  [the longest x1 5.26 us: mirror(): lax.all_to_all(lax.all_to_all(spread, 'row', split_axis=1, concat_axis=0,...]
  transfers between devices with their start and end apart: 20 -> 0, of which waited for: 9 -> 0; matrix products, arithmetic and copies ran while one was open for 8% -> 0% of each run, Pallas kernels for 0% -> 0%
where the time goes in v1:
time: 131 us
  Pallas kernels  122 us (93%)
  local copies, waits for them, and re-layouts  7.8 us (6%)
    pallas_call x1, Pallas kernels, per_device(): pl.pallas_call(functools.partial(kernel, (nr, nc, rows, cols, width, list...  122 us
    unnamed x5, local copies, waits for them, and re-layouts  7.8 us

profile of v1, /device:TPU:3, one launch (start us, length us, event | category | flops | bytes accessed | tf_op | source)
XLA Modules:
  0.0 130.8 jit_solution(5067978627659260677)
XLA Ops:
  0.6 1.3 %copy.9.count = s32[4,2]{1,0:T(4,128)} copy(s32[4,2]{0,1:T(2,128)} %param.10) | data formatting | bytes 64 | tf_op args[3]
  2.0 1.4 %copy.10.coupling = f32[16,8]{1,0:T(8,128)} copy(f32[16,8]{0,1:T(8,128)} %param.12) | data formatting | bytes 1024 | tf_op args[5]
  3.3 1.4 %copy.11.nbr = s32[16,8]{1,0:T(8,128)} copy(s32[16,8]{0,1:T(8,128)} %param.13) | data formatting | bytes 1024 | tf_op args[6]
  4.7 122.4 %sweeps.1 = (f32[4,2,128,128]{3,2,1,0:T(8,128)}, f32[4,2,128,128]{3,2,1,0:T(8,128)}) custom-call(f32[4,2,128,128]{3,2,1,0:T(8,128)} %exch.1, bf16[4,2,2,8,128,128]{5,4,3,2,1,0:T(8,128)(2,1)} %marg_hbm.1, f32[4,2,128]{2,1,0:T(2,128)} %energy.1, s32[4,2]{1,0:T(4,128)} %copy.9.count, f32[16]{0:T(128)} %occ.1, f32[16,8]{1,0:T(8,128)} %copy.10.coupling, ...), custom_call_target="tpu_custom_call" | custom-call | tf_op jit(solution)/shard_map/sweeps/pallas_call | solution.py:339
  127.1 1.9 %copy.14 = f32[4,2,128,128]{3,2,1,0:T(8,128)} copy(f32[4,2,128,128]{3,2,1,0:T(8,128)} %get-tuple-element.4) | data formatting | bytes 1048576
  128.9 1.9 %copy.15 = f32[4,2,128,128]{3,2,1,0:T(8,128)} copy(f32[4,2,128,128]{3,2,1,0:T(8,128)} %get-tuple-element.5) | data formatting | bytes 1048576

commit v2 on v1

--- a/solution.py
+++ b/solution.py
@@ -156,9 +156,8 @@
     def _():
         pl.semaphore_wait(barrier, amount)
 
-    for phase in range(2):
-        for b in range(nc):
-            mirror_start(phase, b)
+    for b in range(nc):
+        mirror_start(0, b)
 
     def reflection(phase, i, j):
         return mirrored[phase, i // nc, lax.rem(i, nc), j].astype(F32).T
@@ -246,13 +245,13 @@
         def body(j, carry):
             two_sided(col_bufs[s][i], 1, i, j, c * nc + j, cside.place)
             return carry
-        lax.fori_loop(0, nc, body, 0)
+        lax.fori_loop(0, nc, body, 0, unroll=True)
 
     def row_products(s, j):
         def body(i, carry):
             two_sided(row_bufs[s][j], 0, i, j, r * nr + i, rside.place)
             return carry
-        lax.fori_loop(0, nr, body, 0)
+        lax.fori_loop(0, nr, body, 0, unroll=2)
 
     def own_slot(side, local):
         return side.own() * side.amount + local
@@ -279,11 +278,9 @@
             row_first(s, j)
         if s == 0:
             load.wait()
-            for b in range(nc):
-                mirror_wait(1, b)
             for i in range(nr):
                 for j in range(nc):
-                    both[i, j] = both[i, j] + (reflection(0, i, j) + reflection(1, i, j))
+                    both[i, j] = both[i, j] + reflection(0, i, j)
         for t in range(nr + 2):
             if t < nr:
                 col_second(s, t)
@@ -294,12 +291,21 @@
             if t >= 2:
                 col_last(s, t - 2)
                 col_products(s, t - 2)
+        if s == 0:
+            for b in range(nc):
+                mirror_start(1, b)
         for j in range(nc):
             row_last(s, j)
             row_products(s, j)
             for i in range(nr):
                 sent[s + 2, i // nc, j, i % nc] = (coup[i, j] * weight[i, j]).astype(BF16)
             mirror_start(s + 2, j)
+        if s == 0:
+            for b in range(nc):
+                mirror_wait(1, b)
+            for i in range(nr):
+                for j in range(nc):
+                    both[i, j] = both[i, j] + reflection(1, i, j)
 
     for i in range(nr):
         for j in range(nc):

time: 131 us -> 134 us (1.023)
  Pallas kernels: 122 us -> 125 us
    pallas_call x1, Pallas kernels: 122 us -> 125 us  [per_device(): pl.pallas_call(functools.partial(kernel, (nr, nc, rows, cols, width, list...]
where the time goes in v2:
time: 134 us
  Pallas kernels  125 us (93%)
  local copies, waits for them, and re-layouts  7.8 us (6%)
    pallas_call x1, Pallas kernels, per_device(): pl.pallas_call(functools.partial(kernel, (nr, nc, rows, cols, width, list...  125 us
    unnamed x5, local copies, waits for them, and re-layouts  7.8 us

profile of v2, /device:TPU:3, one launch (start us, length us, event | category | flops | bytes accessed | tf_op | source)
XLA Modules:
  0.0 133.6 jit_solution(16478919048745313124)
XLA Ops:
  0.6 1.3 %copy.9.count = s32[4,2]{1,0:T(4,128)} copy(s32[4,2]{0,1:T(2,128)} %param.10) | data formatting | bytes 64 | tf_op args[3]
  2.0 1.4 %copy.10.coupling = f32[16,8]{1,0:T(8,128)} copy(f32[16,8]{0,1:T(8,128)} %param.12) | data formatting | bytes 1024 | tf_op args[5]
  3.3 1.4 %copy.11.nbr = s32[16,8]{1,0:T(8,128)} copy(s32[16,8]{0,1:T(8,128)} %param.13) | data formatting | bytes 1024 | tf_op args[6]
  4.7 125.2 %sweeps.1 = (f32[4,2,128,128]{3,2,1,0:T(8,128)}, f32[4,2,128,128]{3,2,1,0:T(8,128)}) custom-call(f32[4,2,128,128]{3,2,1,0:T(8,128)} %exch.1, bf16[4,2,2,8,128,128]{5,4,3,2,1,0:T(8,128)(2,1)} %marg_hbm.1, f32[4,2,128]{2,1,0:T(2,128)} %energy.1, s32[4,2]{1,0:T(4,128)} %copy.9.count, f32[16]{0:T(128)} %occ.1, f32[16,8]{1,0:T(8,128)} %copy.10.coupling, ...), custom_call_target="tpu_custom_call" | custom-call | tf_op jit(solution)/shard_map/sweeps/pallas_call | solution.py:345
  129.9 1.9 %copy.14 = f32[4,2,128,128]{3,2,1,0:T(8,128)} copy(f32[4,2,128,128]{3,2,1,0:T(8,128)} %get-tuple-element.4) | data formatting | bytes 1048576
  131.8 1.9 %copy.15 = f32[4,2,128,128]{3,2,1,0:T(8,128)} copy(f32[4,2,128,128]{3,2,1,0:T(8,128)} %get-tuple-element.5) | data formatting | bytes 1048576
